TPU v7x, 512 devices: a whole 4x4x16 slice. The times are simulated.
512 devices in a mesh: row: 16 (over x, y), col: 32 (over z, core).
Axes of the slice: x: 4, y: 4, z: 16, core: 2. Of those that a mesh axis runs over, the one named last changes fastest.
Arguments:
- start_vector: bfloat16 [4, 2048, 2048], P(None, 'row', 'col'), may hold values from -150 to 150
- left_env: bfloat16 [5, 2048, 2048], P(None, 'row', 'col'), may hold values from -5 to 6
- right_env: bfloat16 [5, 2048, 2048], P(None, 'col', 'row'), may hold values from -5 to 6
- left_tensor: float32 [5, 5, 2, 2], replicated, may hold values from -1.5 to 2.5
- right_tensor: float32 [5, 5, 2, 2], replicated, may hold values from -1.5 to 2.5
Outputs:
- next_vector: bfloat16 [4, 2048, 2048], P(None, 'row', 'col')
- coefficients: float32 [2], replicated
All inputs are finite; a program needn't handle non-finite values.
Results may differ from a plain program's by a relative error of at most 0.023.
Values may be sent and summed in bfloat16 or wider, within the bound.
No kernel may reach another device: no remote copies, remote signals or barrier semaphores. Data moves between devices by JAX's collectives and lax.ppermute only.
A program may use at most 64 MiB of HBM per device.

v0:
```python
import jax
import jax.numpy as jnp
from jax import lax
from jax.sharding import Mesh
from jax.sharding import PartitionSpec as P

ROW = ("row_0", "row_1")
COL = ("col_0", "col_1")
ROW_COL = ("row_0", "row_1", "col_0", "col_1")
epsilon = 1e-06


def copy_for_each(x, axis):
    size = lax.axis_size(axis)
    return lax.all_to_all(jnp.broadcast_to(x[None], (size, *x.shape)), axis, 0, 0, tiled=True)


def joined_along(pieces, dim):
    pieces = jnp.moveaxis(pieces, 0, dim)
    lengths = pieces.shape
    return pieces.reshape(*lengths[:dim], lengths[dim] * lengths[dim + 1], *lengths[dim + 2 :])


def gathered_copies(x, axis, dim):
    pieces = copy_for_each(x, axis)
    return joined_along(pieces, dim)


def sum_in_order(pieces, axes, sequence):
    lengths = [lax.axis_size(a) for a in axes]
    pieces = pieces.reshape(*lengths, *pieces.shape[1:])
    pieces = pieces.transpose(*sequence, *range(len(axes), pieces.ndim))
    pieces = pieces.reshape(-1, *pieces.shape[len(axes) :])
    for k in sequence:
        pieces = lax.psum_scatter(pieces, axes[k], scatter_dimension=0, tiled=True)
    return pieces[0]


def cut_along(x, dim, size):
    lengths = x.shape
    pieces = x.reshape(*lengths[:dim], size, lengths[dim] // size, *lengths[dim + 1 :])
    return jnp.moveaxis(pieces, dim, 0)


def scatter_axes(x, axes, sequence, dim):
    size = lax.axis_size(axes)
    return sum_in_order(cut_along(x, dim, size), axes, sequence)


def by_axis(x, axes):
    for axis in axes:
        x = lax.psum(x, axis)
    return x


def coupling(left_tensor, right_tensor):
    channels = left_tensor.shape[0]
    joined = jnp.einsum(
        "wuac,uvbd->vabwcd", left_tensor, right_tensor, precision=lax.Precision.HIGHEST
    )
    return joined.reshape(channels, 4, channels, 4)


def contract_left(portion, columns):
    return jnp.einsum("wax,txb->wtba", portion, columns, preferred_element_type=jnp.float32)


def mix_channels(coupling_table, cross):
    mixed_bond = jnp.einsum(
        "vswt,wtba->vsba", coupling_table, cross, precision=lax.Precision.HIGHEST
    )
    return mixed_bond.astype(jnp.bfloat16)


def contract_right(mixed_bond, portion):
    return jnp.einsum("vsba,vbc->sac", mixed_bond, portion, preferred_element_type=jnp.float32)


def apply_hamiltonian(vector, coupling_table, panels):
    columns = gathered_copies(vector, ROW, 1)
    cross = contract_left(panels[0], columns)
    mixed_bond = mix_channels(coupling_table, cross)
    partials = contract_right(mixed_bond, panels[1])
    return scatter_axes(partials.astype(jnp.bfloat16), COL, (1, 0), 2).astype(jnp.float32)


def local_mean(former, latter, entries):
    return jnp.sum(former * latter) / entries


def body(start_vector, left_env, right_env, left_tensor, right_tensor):
    coupling_table = coupling(left_tensor, right_tensor)
    entries = float(
        start_vector.shape[0]
        * start_vector.shape[1]
        * start_vector.shape[2]
        * lax.axis_size(ROW)
        * lax.axis_size(COL)
    )
    panels = (lax.all_gather(left_env, COL, axis=2, tiled=True), gathered_copies(right_env, ROW, 2))
    base_vector = start_vector.astype(jnp.float32)
    image = apply_hamiltonian(start_vector, coupling_table, panels)
    base_square, correlation, image_square = (
        by_axis(local_mean(base_vector, base_vector, entries), ROW_COL),
        by_axis(local_mean(base_vector, image, entries), ROW_COL),
        by_axis(local_mean(image, image, entries), ROW_COL),
    )
    alpha = correlation / (base_square + epsilon)
    residual = image - alpha * base_vector
    rho = jnp.sqrt(image_square - 2.0 * alpha * correlation + alpha * alpha * base_square + epsilon)
    next_vector = (residual / rho).astype(jnp.bfloat16)
    coefficients = jnp.stack([alpha, rho])
    return (next_vector, coefficients)


def solution(mesh):
    finer = Mesh(mesh.devices.reshape(4, 4, 16, 2), ("row_0", "row_1", "col_0", "col_1"))
    in_specs = (P(None, ROW, COL), P(None, ROW, COL), P(None, COL, ROW), P(), P())
    out_specs = (P(None, ROW, COL), P())
    return jax.shard_map(body, mesh=finer, in_specs=in_specs, out_specs=out_specs, check_vma=False)
```

profile of v0, /device:TPU:1, one launch (start us, length us, event | category | flops | bytes accessed | tf_op | source)
XLA Modules:
  0.0 263.9 jit_solution(11655160880378192590)
XLA Ops:
  7.2 0.0 copy-start
  7.2 0.0 copy-start.2
  7.2 0.0 all-gather.2.cloned.1.call-start
  7.2 0.7 all-gather.2.cloned.1.call-update
  7.9 1.1 broadcast_in_dim.4
  9.0 22.4 %all_to_all.10 = bf16[16,4,128,64]{2,3,1,0:T(8,128)(2,1)S(1)} all-to-all(bf16[16,4,128,64]{2,3,1,0:T(8,128)(2,1)S(1)} %broadcast_in_dim.4), channel_id=1, replica_groups=mesh['row_0'=4,'row_1'=4,'col_0'=16,'col_1'=2] {'row_0','row_1'}, dimensions={0} | all-to-all | bytes 2097152 | tf_op jit(solution)/shard_map/all_to_all | solution.py:15
  31.4 0.0 copy-done.2
  31.4 0.0 copy-start.3
  31.4 1.4 broadcast_in_dim.5
  32.8 3.7 %all-to-all-start.1 = ((bf16[16,5,64,128]{3,2,1,0:T(8,128)(2,1)}), bf16[16,5,64,128]{3,2,1,0:T(8,128)(2,1)S(1)}, u32[]{:S(2)}, u32[]{:S(2)}) async-start(bf16[16,5,64,128]{3,2,1,0:T(8,128)(2,1)} %broadcast_in_dim.5), calls=%async_computation.1 | async-start | bytes 2621440 | tf_op jit(solution)/shard_map/all_to_all | solution.py:15
  36.5 0.0 reduce-scatter.3.cloned.1.call-start
  36.6 0.0 copy-done
  36.6 0.0 copy-done.3
  36.6 0.4 convolution_bitcast_fusion.1
  37.0 0.7 copy.19
  37.7 1.3 reshape.35
  39.0 14.3 %all-to-all-done.1 = bf16[16,5,64,128]{3,2,1,0:T(8,128)(2,1)S(1)} async-done(((bf16[16,5,64,128]{3,2,1,0:T(8,128)(2,1)}), bf16[16,5,64,128]{3,2,1,0:T(8,128)(2,1)S(1)}, u32[]{:S(2)}, u32[]{:S(2)}) %all-to-all-start.1) | async-done | bytes 1310752 | tf_op jit(solution)/shard_map/all_to_all | solution.py:15
  53.3 0.9 copy.22
  54.2 0.6 reshape.40
  54.8 33.2 %all-gather.2.cloned.1.call-done = bf16[5,128,2048]{1,2,0:T(8,128)(2,1)} async-done(((bf16[5,128,64]{1,2,0:T(8,128)(2,1)}), bf16[5,128,2048]{1,2,0:T(8,128)(2,1)}) %all-gather.2.cloned.1.call-update) | async-done | bytes 2621456 | tf_op jit(solution)/shard_map/all_gather | solution.py:100
  88.0 3.0 %fusion.3 = f32[5,4,64,128]{3,2,0,1:T(8,128)S(1)} fusion(bf16[5,128,2048]{1,2,0:T(8,128)(2,1)} %all-gather.2.cloned.1.call-done, bf16[4,2048,64,1]{1,2,0,3:T(8,128)(2,1)} %reshape.35), kind=kOutput, calls=%fused_computation.5 | convolution fusion | flops 671088640 | bytes 4325376 | tf_op jit(solution)/shard_map/wax,txb->wtba/dot_general | solution.py:65
  91.1 4.0 %fusion.2 = bf16[5,4,64,128]{3,0,2,1:T(8,128)(2,1)S(1)} fusion(f32[5,4,64,128]{3,2,0,1:T(8,128)S(1)} %fusion.3, f32[5,4,5,4,1]{2,3,1,0,4:T(4,128)S(1)} %bitcast.57), kind=kOutput, calls=%fused_computation.4 | convolution fusion | flops 39485440 | bytes 984640 | tf_op jit(solution)/shard_map/vswt,wtba->vsba/dot_general | solution.py:69
  95.1 1.3 bitcast_convert_fusion
  96.4 2.5 copy.24
  98.9 3.2 %copy.25 = bf16[2,16,4,128,64]{3,4,2,1,0:T(8,128)(2,1)} copy(bf16[2,16,4,128,64]{3,4,0,1,2:T(8,128)(2,1)} %bitcast.54) | data formatting | bytes 4194304 | tf_op jit(solution)/shard_map/transpose | solution.py:32
  102.1 0.0 copy-start.1
  102.1 0.0 reduce-scatter.3.cloned.1.call-update
  102.1 0.0 reduce-scatter.5.cloned.1.call-start
  102.1 17.6 %reduce-scatter.3.cloned.1.call-done = bf16[16,4,128,64]{2,3,1,0:T(8,128)(2,1)} async-done(((bf16[32,4,128,64]{2,3,1,0:T(8,128)(2,1)}), bf16[16,4,128,64]{2,3,1,0:T(8,128)(2,1)}) %reduce-scatter.3.cloned.1.call-update) | async-done | bytes 1048592 | tf_op jit(solution)/shard_map/reduce_scatter | solution.py:35
  119.8 0.0 reduce-scatter.5.cloned.1.call-update
  119.8 64.3 %reduce-scatter.5.cloned.1.call-done = bf16[1,4,128,64]{2,3,1,0:T(8,128)(2,1)} async-done(((bf16[16,4,128,64]{2,3,1,0:T(8,128)(2,1)}), bf16[1,4,128,64]{2,3,1,0:T(8,128)(2,1)}) %reduce-scatter.5.cloned.1.call-update) | async-done | bytes 65552 | tf_op jit(solution)/shard_map/reduce_scatter | solution.py:35
  184.0 0.0 copy-done.1
  184.0 1.5 fusion.10
  187.5 9.5 %all-reduce.2 = (f32[]{:T(128)}, f32[]{:T(128)}, f32[]{:T(128)}) all-reduce(f32[]{:T(128)S(6)} %div.21, f32[]{:T(128)S(6)} %div.18, f32[]{:T(128)S(6)} %div.19), channel_id=1, replica_groups=mesh['row_0'=4,'row_1'=4,'col_0'=16,'col_1'=2] {'row_0'}, use_global_device_ids=true, to_apply=%region_13.0 | all-reduce | flops 3 | bytes 24 | tf_op jit(solution)/shard_map/psum | solution.py:52
  196.9 8.5 %all-reduce.1 = (f32[]{:T(128)}, f32[]{:T(128)}, f32[]{:T(128)}) all-reduce(f32[]{:T(128)} %get-tuple-element.11, f32[]{:T(128)} %get-tuple-element.12, f32[]{:T(128)} %get-tuple-element.13), channel_id=1, replica_groups=mesh['row_0'=4,'row_1'=4,'col_0'=16,'col_1'=2] {'row_1'}, use_global_device_ids=true, to_apply=%region_14.0 | all-reduce | flops 3 | bytes 24 | tf_op jit(solution)/shard_map/psum | solution.py:52
  205.5 22.2 %all-reduce = (f32[]{:T(128)}, f32[]{:T(128)}, f32[]{:T(128)}) all-reduce(f32[]{:T(128)} %get-tuple-element.8, f32[]{:T(128)} %get-tuple-element.9, f32[]{:T(128)} %get-tuple-element.10), channel_id=1, replica_groups=mesh['row_0'=4,'row_1'=4,'col_0'=16,'col_1'=2] {'col_0'}, use_global_device_ids=true, to_apply=%region_15.0 | all-reduce | flops 3 | bytes 24 | tf_op jit(solution)/shard_map/psum | solution.py:52
  227.7 24.4 %all-reduce.3 = (f32[]{:T(128)}, f32[]{:T(128)}, f32[]{:T(128)}) all-reduce(f32[]{:T(128)} %get-tuple-element.5, f32[]{:T(128)} %get-tuple-element.6, f32[]{:T(128)} %get-tuple-element.7), channel_id=1, replica_groups=mesh['row_0'=4,'row_1'=4,'col_0'=16,'col_1'=2] {'col_1'}, use_global_device_ids=true, to_apply=%region_16.0 | all-reduce | flops 3 | bytes 24 | tf_op jit(solution)/shard_map/psum | solution.py:52
  255.3 0.6 pad_maximum_fusion
  255.8 1.5 fusion.13
  (1 shorter events, 0.0 us)
Async XLA Ops:
  7.2 29.4 %copy-start = (f32[5,5,2,2]{1,3,2,0:T(2,128)S(1)}, f32[5,5,2,2]{1,3,2,0:T(2,128)}, u32[]{:S(2)}) copy-start(f32[5,5,2,2]{1,3,2,0:T(2,128)} %param.8) | copy-start | bytes 1204
  7.2 24.2 %copy-start.2 = (bf16[5,64,128]{2,1,0:T(8,128)(2,1)S(1)}, bf16[5,64,128]{2,1,0:T(8,128)(2,1)}, u32[]{:S(2)}) copy-start(bf16[5,64,128]{2,1,0:T(8,128)(2,1)} %param.7) | copy-start | bytes 245764
  7.2 80.8 %all-gather.2.cloned.1.call-start = ((), (), s32[]{:S(2)}) async-start(), calls=%async_computation.4 | async-start | bytes 2703360 | tf_op jit(solution)/shard_map/all_gather | solution.py:100
  31.4 5.2 %copy-start.3 = (f32[5,5,2,2]{1,3,2,0:T(2,128)S(1)}, f32[5,5,2,2]{1,3,2,0:T(2,128)}, u32[]{:S(2)}) copy-start(f32[5,5,2,2]{1,3,2,0:T(2,128)} %param.9) | copy-start | bytes 1204
  32.8 20.5 %all-to-all-start.1 = ((bf16[16,5,64,128]{3,2,1,0:T(8,128)(2,1)}), bf16[16,5,64,128]{3,2,1,0:T(8,128)(2,1)S(1)}, u32[]{:S(2)}, u32[]{:S(2)}) async-start(bf16[16,5,64,128]{3,2,1,0:T(8,128)(2,1)} %broadcast_in_dim.5), calls=%async_computation.1 | async-start | bytes 2621440 | tf_op jit(solution)/shard_map/all_to_all | solution.py:15
  36.5 83.2 %reduce-scatter.3.cloned.1.call-start = ((), (), s32[]{:S(2)}) async-start(), calls=%async_computation.5 | async-start | bytes 3145728 | tf_op jit(solution)/shard_map/reduce_scatter | solution.py:35
  102.1 82.0 %copy-start.1 = (bf16[4,128,64]{1,2,0:T(8,128)(2,1)S(1)}, bf16[4,128,64]{1,2,0:T(8,128)(2,1)}, u32[]{:S(2)}) copy-start(bf16[4,128,64]{1,2,0:T(8,128)(2,1)} %param.5) | copy-start | bytes 196612
  102.1 82.0 %reduce-scatter.5.cloned.1.call-start = ((), (), s32[]{:S(2)}) async-start(), calls=%async_computation.6 | async-start | bytes 1114112 | tf_op jit(solution)/shard_map/reduce_scatter | solution.py:35
Sparse Core Ops, SparseCore 0:
  10.1 77.8 all-gather.1
  102.2 17.5 reduce-scatter.2
  122.6 61.4 reduce-scatter.4
where the time goes:
time: 264 us
  waiting for transfers between devices  130 us (49%)
  blocking collectives  87.1 us (33%)
  between operations  18.9 us (7%)
  local copies, waits for them, and re-layouts  11.7 us (4%)
  matrix products  8.74 us (3%)
  starting transfers between devices  3.82 us (1%)
  other arithmetic  3.6 us (1%)
    reduce_scatter x2, waiting for transfers between devices, sum_in_order(): pieces = lax.psum_scatter(pieces, axes[k], scatter_dimension=0, tiled=True)  81.9 us
    psum x4, blocking collectives, by_axis(): x = lax.psum(x, axis)  64.7 us
    all_gather x1, waiting for transfers between devices, body(): lax.all_gather(left_env, COL, axis=2, tiled=True)  33.2 us
    all_to_all x1, blocking collectives, copy_for_each(): lax.all_to_all(jnp.broadcast_to(x[None], (size, *x.shape)), axis, 0, 0, t...  22.4 us
    all_to_all x1, waiting for transfers between devices, copy_for_each(): lax.all_to_all(jnp.broadcast_to(x[None], (size, *x.shape)), axis, 0, 0, t...  14.3 us
  transfers between devices with their start and end apart: 4, of which 4 were waited for; matrix products, arithmetic and copies ran while one was open for 2% of the time, Pallas kernels for 0%

commit v1 on v0

--- a/solution.py
+++ b/solution.py
@@ -8,6 +8,13 @@
 COL = ("col_0", "col_1")
 ROW_COL = ("row_0", "row_1", "col_0", "col_1")
 epsilon = 1e-06
+
+
+def exchange_gather(value, name, dim):
+    n_dev = lax.axis_size(name)
+    blocks = jnp.stack([value for _ in range(n_dev)])
+    blocks = lax.all_to_all(blocks, name, split_axis=0, concat_axis=0)
+    return jnp.concatenate(blocks, axis=dim)
 
 
 def copy_for_each(x, axis):
@@ -97,7 +104,7 @@
         * lax.axis_size(ROW)
         * lax.axis_size(COL)
     )
-    panels = (lax.all_gather(left_env, COL, axis=2, tiled=True), gathered_copies(right_env, ROW, 2))
+    panels = (exchange_gather(left_env, COL, 2), gathered_copies(right_env, ROW, 2))
     base_vector = start_vector.astype(jnp.float32)
     image = apply_hamiltonian(start_vector, coupling_table, panels)
     base_square, correlation, image_square = (

time: 264 us -> 365 us (1.38)
  waiting for transfers between devices: 130 us -> 185 us
  blocking collectives: 87.1 us -> 106 us
  starting transfers between devices: 3.82 us -> 21.6 us
  local copies, waits for them, and re-layouts: 11.7 us -> 22.3 us
    all_to_all x1, waiting for transfers between devices: 14.3 us -> 107 us  [exchange_gather(): blocks = lax.all_to_all(blocks, name, split_axis=0, concat_axis=0)]
    all_gather x1 -> x0, waiting for transfers between devices: 33.2 us -> none  [body(): lax.all_gather(left_env, COL, axis=2, tiled=True)]
    all_to_all x1 -> x2, blocking collectives: 22.4 us -> 41.5 us  [copy_for_each(): lax.all_to_all(jnp.broadcast_to(x[None], (size, *x.shape)), axis, 0, 0, t...]
    all_to_all x1, starting transfers between devices: 3.7 us -> 21.6 us  [exchange_gather(): blocks = lax.all_to_all(blocks, name, split_axis=0, concat_axis=0)]
    transpose x2, local copies, waits for them, and re-layouts: 1.53 us -> 6.16 us  [joined_along(): pieces = jnp.moveaxis(pieces, 0, dim)]
    reduce_scatter x2, waiting for transfers between devices: 81.9 us -> 77.7 us  [sum_in_order(): pieces = lax.psum_scatter(pieces, axes[k], scatter_dimension=0, tiled=True)]
    reshape x2, local copies, waits for them, and re-layouts: 1.88 us -> 5.53 us  [joined_along(): pieces.reshape(*lengths[:dim], lengths[dim] * lengths[dim + 1], *lengths[...]
  transfers between devices with their start and end apart: 4 -> 3, of which waited for: 4 -> 3; matrix products, arithmetic and copies ran while one was open for 2% -> 3% of each run, Pallas kernels for 0% -> 0%
where the time goes in v1:
time: 365 us; the launch traced here: 364 us
  waiting for transfers between devices  185 us (51%)
  blocking collectives  106 us (29%)
  local copies, waits for them, and re-layouts  22.3 us (6%)
  starting transfers between devices  21.6 us (6%)
  between operations  19.2 us (5%)
  matrix products  6.67 us (2%)
    all_to_all x1, waiting for transfers between devices, exchange_gather(): blocks = lax.all_to_all(blocks, name, split_axis=0, concat_axis=0)  107 us
    reduce_scatter x2, waiting for transfers between devices, sum_in_order(): pieces = lax.psum_scatter(pieces, axes[k], scatter_dimension=0, tiled=True)  77.7 us
    psum x4, blocking collectives, by_axis(): x = lax.psum(x, axis)  64.5 us
    all_to_all x2, blocking collectives, copy_for_each(): lax.all_to_all(jnp.broadcast_to(x[None], (size, *x.shape)), axis, 0, 0, t...  41.5 us
    all_to_all x1, starting transfers between devices, exchange_gather(): blocks = lax.all_to_all(blocks, name, split_axis=0, concat_axis=0)  21.6 us
  transfers between devices with their start and end apart: 3, of which 3 were waited for; matrix products, arithmetic and copies ran while one was open for 3% of the time, Pallas kernels for 0%

profile of v1, /device:TPU:1, one launch (start us, length us, event | category | flops | bytes accessed | tf_op | source)
XLA Modules:
  0.0 364.2 jit_solution(14813103531423550207)
XLA Ops:
  7.2 0.0 copy-start
  7.2 0.0 copy-start.4
  7.2 1.1 broadcast_in_dim.4
  8.3 21.9 %all_to_all.15 = bf16[16,4,128,64]{2,3,1,0:T(8,128)(2,1)} all-to-all(bf16[16,4,128,64]{2,3,1,0:T(8,128)(2,1)S(1)} %broadcast_in_dim.4), channel_id=1, replica_groups=mesh['row_0'=4,'row_1'=4,'col_0'=16,'col_1'=2] {'row_0','row_1'}, dimensions={0} | all-to-all | bytes 2097152 | tf_op jit(solution)/shard_map/all_to_all | solution.py:22
  30.2 0.0 copy-done.4
  30.2 0.0 copy-start.5
  30.2 0.3 broadcast_in_dim.5
  30.5 19.6 %all_to_all.16 = bf16[16,5,64,128]{3,2,1,0:T(8,128)(2,1)} all-to-all(bf16[16,5,64,128]{3,2,1,0:T(8,128)(2,1)S(1)} %broadcast_in_dim.5), channel_id=1, replica_groups=mesh['row_0'=4,'row_1'=4,'col_0'=16,'col_1'=2] {'row_0','row_1'}, dimensions={0} | all-to-all | bytes 2621440 | tf_op jit(solution)/shard_map/all_to_all | solution.py:22
  50.1 0.0 copy-done.5
  50.1 2.2 stack.8
  52.3 0.0 copy-start.6
  52.3 21.6 %all-to-all-start.1 = ((bf16[32,5,128,64]{2,3,1,0:T(8,128)(2,1)}), bf16[32,5,128,64]{2,3,1,0:T(8,128)(2,1)S(1)}, u32[]{:S(2)}, u32[]{:S(2)}) async-start(bf16[32,5,128,64]{2,3,1,0:T(8,128)(2,1)} %stack.8), calls=%async_computation.1 | async-start | bytes 5242880 | tf_op jit(solution)/shard_map/all_to_all | solution.py:16
  73.8 0.0 reduce-scatter.3.cloned.1.call-start
  73.9 0.0 copy-done
  73.9 0.0 copy-done.6
  73.9 0.4 convolution_bitcast_fusion.2
  74.4 2.9 copy.20
  77.3 2.3 reshape.45
  79.6 3.3 copy.25
  82.8 3.2 reshape.50
  86.0 107.2 %all-to-all-done.1 = bf16[32,5,128,64]{2,3,1,0:T(8,128)(2,1)S(1)} async-done(((bf16[32,5,128,64]{2,3,1,0:T(8,128)(2,1)}), bf16[32,5,128,64]{2,3,1,0:T(8,128)(2,1)S(1)}, u32[]{:S(2)}, u32[]{:S(2)}) %all-to-all-start.1) | async-done | bytes 2621472 | tf_op jit(solution)/shard_map/all_to_all | solution.py:16
  193.3 0.0 copy-start.2
  193.3 0.6 copy.21
  193.8 0.7 copy-done.2
  194.5 0.0 copy-start.1
  194.5 1.0 convolution_bitcast_fusion.1
  195.5 4.0 %fusion = bf16[5,4,64,128]{3,0,2,1:T(8,128)(2,1)S(1)} fusion(f32[5,4,64,128]{3,2,0,1:T(8,128)S(1)} %convolution_bitcast_fusion.1, f32[5,4,5,4,1]{2,3,1,0,4:T(4,128)S(1)} %bitcast.59), kind=kOutput, calls=%fused_computation.2 | convolution fusion | flops 39485440 | bytes 984640 | tf_op jit(solution)/shard_map/vswt,wtba->vsba/dot_general | solution.py:76
  199.5 0.0 copy-done.1
  199.5 1.3 bitcast_convert_fusion
  200.8 2.5 copy.27
  203.3 3.2 copy.28
  206.5 0.0 copy-start.3
  206.5 0.0 reduce-scatter.3.cloned.1.call-update
  206.5 0.0 reduce-scatter.5.cloned.1.call-start
  206.5 13.2 %reduce-scatter.3.cloned.1.call-done = bf16[16,4,128,64]{2,3,1,0:T(8,128)(2,1)} async-done(((bf16[32,4,128,64]{2,3,1,0:T(8,128)(2,1)}), bf16[16,4,128,64]{2,3,1,0:T(8,128)(2,1)}) %reduce-scatter.3.cloned.1.call-update) | async-done | bytes 1048592 | tf_op jit(solution)/shard_map/reduce_scatter | solution.py:42
  219.7 0.0 reduce-scatter.5.cloned.1.call-update
  219.8 64.5 %reduce-scatter.5.cloned.1.call-done = bf16[1,4,128,64]{2,3,1,0:T(8,128)(2,1)} async-done(((bf16[16,4,128,64]{2,3,1,0:T(8,128)(2,1)}), bf16[1,4,128,64]{2,3,1,0:T(8,128)(2,1)}) %reduce-scatter.5.cloned.1.call-update) | async-done | bytes 65552 | tf_op jit(solution)/shard_map/reduce_scatter | solution.py:42
  284.2 0.0 copy-done.3
  284.2 1.5 fusion.5
  287.7 8.7 %all-reduce.2 = (f32[]{:T(128)}, f32[]{:T(128)}, f32[]{:T(128)}) all-reduce(f32[]{:T(128)S(6)} %div.21, f32[]{:T(128)S(6)} %div.18, f32[]{:T(128)S(6)} %div.19), channel_id=1, replica_groups=mesh['row_0'=4,'row_1'=4,'col_0'=16,'col_1'=2] {'row_0'}, use_global_device_ids=true, to_apply=%region_13.0 | all-reduce | flops 3 | bytes 24 | tf_op jit(solution)/shard_map/psum | solution.py:59
  296.4 9.5 %all-reduce.1 = (f32[]{:T(128)}, f32[]{:T(128)}, f32[]{:T(128)}) all-reduce(f32[]{:T(128)} %get-tuple-element.11, f32[]{:T(128)} %get-tuple-element.12, f32[]{:T(128)} %get-tuple-element.13), channel_id=1, replica_groups=mesh['row_0'=4,'row_1'=4,'col_0'=16,'col_1'=2] {'row_1'}, use_global_device_ids=true, to_apply=%region_14.0 | all-reduce | flops 3 | bytes 24 | tf_op jit(solution)/shard_map/psum | solution.py:59
  305.9 21.8 %all-reduce = (f32[]{:T(128)}, f32[]{:T(128)}, f32[]{:T(128)}) all-reduce(f32[]{:T(128)} %get-tuple-element.8, f32[]{:T(128)} %get-tuple-element.9, f32[]{:T(128)} %get-tuple-element.10), channel_id=1, replica_groups=mesh['row_0'=4,'row_1'=4,'col_0'=16,'col_1'=2] {'col_0'}, use_global_device_ids=true, to_apply=%region_15.0 | all-reduce | flops 3 | bytes 24 | tf_op jit(solution)/shard_map/psum | solution.py:59
  327.7 24.5 %all-reduce.3 = (f32[]{:T(128)}, f32[]{:T(128)}, f32[]{:T(128)}) all-reduce(f32[]{:T(128)} %get-tuple-element.5, f32[]{:T(128)} %get-tuple-element.6, f32[]{:T(128)} %get-tuple-element.7), channel_id=1, replica_groups=mesh['row_0'=4,'row_1'=4,'col_0'=16,'col_1'=2] {'col_1'}, use_global_device_ids=true, to_apply=%region_16.0 | all-reduce | flops 3 | bytes 24 | tf_op jit(solution)/shard_map/psum | solution.py:59
  355.3 0.6 pad_maximum_fusion
  355.9 1.5 fusion.8
  (1 shorter events, 0.0 us)
Async XLA Ops:
  7.2 66.7 %copy-start = (f32[5,5,2,2]{1,3,2,0:T(2,128)S(1)}, f32[5,5,2,2]{1,3,2,0:T(2,128)}, u32[]{:S(2)}) copy-start(f32[5,5,2,2]{1,3,2,0:T(2,128)} %param.8) | copy-start | bytes 1204
  7.2 23.0 %copy-start.4 = (bf16[5,64,128]{2,1,0:T(8,128)(2,1)S(1)}, bf16[5,64,128]{2,1,0:T(8,128)(2,1)}, u32[]{:S(2)}) copy-start(bf16[5,64,128]{2,1,0:T(8,128)(2,1)} %param.7) | copy-start | bytes 245764
  30.2 19.9 %copy-start.5 = (bf16[5,128,64]{1,2,0:T(8,128)(2,1)S(1)}, bf16[5,128,64]{1,2,0:T(8,128)(2,1)}, u32[]{:S(2)}) copy-start(bf16[5,128,64]{1,2,0:T(8,128)(2,1)} %param.6) | copy-start | bytes 245764
  52.3 21.6 %copy-start.6 = (f32[5,5,2,2]{1,3,2,0:T(2,128)S(1)}, f32[5,5,2,2]{1,3,2,0:T(2,128)}, u32[]{:S(2)}) copy-start(f32[5,5,2,2]{1,3,2,0:T(2,128)} %param.9) | copy-start | bytes 1204
  52.3 141.0 %all-to-all-start.1 = ((bf16[32,5,128,64]{2,3,1,0:T(8,128)(2,1)}), bf16[32,5,128,64]{2,3,1,0:T(8,128)(2,1)S(1)}, u32[]{:S(2)}, u32[]{:S(2)}) async-start(bf16[32,5,128,64]{2,3,1,0:T(8,128)(2,1)} %stack.8), calls=%async_computation.1 | async-start | bytes 5242880 | tf_op jit(solution)/shard_map/all_to_all | solution.py:16
  73.8 145.9 %reduce-scatter.3.cloned.1.call-start = ((), (), s32[]{:S(2)}) async-start(), calls=%async_computation.5 | async-start | bytes 3145728 | tf_op jit(solution)/shard_map/reduce_scatter | solution.py:42
  193.3 1.2 copy-start.2
  194.5 5.0 %copy-start.1 = (bf16[5,64,2048,1]{2,1,0,3:T(8,128)(2,1)S(1)}, bf16[5,64,2048,1]{2,1,0,3:T(8,128)(2,1)}, u32[]{:S(2)}) copy-start(bf16[5,64,2048,1]{2,1,0,3:T(8,128)(2,1)} %reshape.50) | copy-start | bytes 3932164
  206.5 77.8 %copy-start.3 = (bf16[4,128,64]{1,2,0:T(8,128)(2,1)S(1)}, bf16[4,128,64]{1,2,0:T(8,128)(2,1)}, u32[]{:S(2)}) copy-start(bf16[4,128,64]{1,2,0:T(8,128)(2,1)} %param.5) | copy-start | bytes 196612
  206.5 77.7 %reduce-scatter.5.cloned.1.call-start = ((), (), s32[]{:S(2)}) async-start(), calls=%async_computation.6 | async-start | bytes 1114112 | tf_op jit(solution)/shard_map/reduce_scatter | solution.py:42
Sparse Core Ops, SparseCore 0:
  206.6 13.0 reduce-scatter.2
  222.5 61.6 reduce-scatter.4
